TPU v7x, 256 devices: a whole 4x4x8 slice. The times are simulated.
256 devices in a mesh: rows: 64 (over x, z, core), grp: 4 (over y).
Axes of the slice: x: 4, y: 4, z: 8, core: 2. Of those that a mesh axis runs over, the one named last changes fastest.
Arguments:
- matrix: bfloat16 [81920, 16384], P(('rows', 'grp')), may hold values from -36 to 36
- sample_rows: int32 [256, 128, 256], P(('rows', 'grp')), may hold values from 0 to 319
- pair_list: int32 [64, 64, 4], replicated, may hold values from 0 to 2047, as said below
- pair_count: int32 [64, 64], replicated, may hold values from 1 to 4, as said below
- pair_blocks: int32 [2048, 2], replicated, may hold values from 0 to 127, as said below
Outputs:
- gram: float32 [2048, 128, 128], P(('rows', 'grp'))
Inputs may be any that keep to these rules, and one draw needn't show every extreme that they name: `pair_list`: entry [s, r, k] lies in [r * 32, (r + 1) * 32); the 4 entries of one [s, r] are distinct. `pair_count`: every row group has some owner with all 4 slots active, and some owner has all 4 slots active from every row group. `pair_blocks`: the two blocks of a pair differ.
All inputs are finite; a program needn't handle non-finite values.
Results may differ from a plain program's by a relative error of at most 0.0016.
Values sent between devices are 32-bit elements; how exact they have to be, the bound alone decides.
A program may use at most 192 MiB of HBM per device.

v0:
```python
import math

import jax
import jax.numpy as jnp
from jax import lax
from jax.sharding import PartitionSpec as P

epsilon = 1e-06


def total_of_pieces(x, axis):
    pieces = lax.all_gather(x, axis)
    return pieces.sum(axis=0)


def cut_along(x, dim, count):
    shape = x.shape
    pieces = x.reshape(*shape[:dim], count, shape[dim] // count, *shape[dim + 1 :])
    return jnp.moveaxis(pieces, dim, 0)


def summed_on_arrival(x, axis, dim):
    pieces = cut_along(x, dim, lax.axis_size(axis))
    arrived = lax.all_to_all(pieces, axis, split_axis=0, concat_axis=0, tiled=True)
    return arrived.sum(axis=0)


def shards(matrix, sample_rows, pair_list, pair_count, pair_blocks):
    rows_dev, column_count = matrix.shape
    block_count = sample_rows.shape[1]
    sample_count = sample_rows.shape[2]
    width = column_count // block_count
    row_axis_size = lax.axis_size("rows")
    grp_axis_size = lax.axis_size("grp")
    slot_cap = pair_list.shape[2]
    region_size = pair_blocks.shape[0] // row_axis_size
    row_index = lax.axis_index("rows")
    grp_index = lax.axis_index("grp")
    squares = jnp.sum(jnp.square(matrix.astype(jnp.float32)), axis=0)
    column_total = total_of_pieces(squares, ("rows", "grp"))
    root_mean = jnp.sqrt(column_total / (rows_dev * row_axis_size * grp_axis_size) + epsilon)
    positions = lax.iota(jnp.int32, rows_dev)
    picked = sample_rows[0]
    multiplicity = jnp.sum(
        (picked[:, :, None] == positions[None, None, :]).astype(jnp.float32), axis=1
    )
    blocks = matrix.reshape(rows_dev, block_count, width)
    weighted = (jnp.transpose(multiplicity)[:, :, None] * blocks.astype(jnp.float32)).astype(
        jnp.bfloat16
    )
    my_pairs = pair_list[row_index]
    my_counts = pair_count[row_index]
    live_mask = (lax.iota(jnp.int32, slot_cap)[None, :] < my_counts[:, None]).astype(jnp.float32)
    pair_ids = my_pairs.reshape(-1)
    slot_total = pair_ids.shape[0]
    group_size = math.gcd(32, slot_total)
    first_block = jnp.take(pair_blocks[:, 0], pair_ids).reshape(-1, group_size)
    second_block = jnp.take(pair_blocks[:, 1], pair_ids).reshape(-1, group_size)

    def tile_group(block_pair):
        weighted_cols = jnp.take(weighted, block_pair[0], axis=1)
        plain_cols = jnp.take(blocks, block_pair[1], axis=1)
        return jnp.einsum(
            "rgi,rgj->gij", weighted_cols, plain_cols, preferred_element_type=jnp.float32
        )

    partial_tiles = lax.map(tile_group, (first_block, second_block))
    partial_tiles = (
        partial_tiles.reshape(row_axis_size, slot_cap, width, width) * live_mask[:, :, None, None]
    )
    share_size = slot_cap // grp_axis_size
    reduced = summed_on_arrival(partial_tiles, "grp", 1)
    received = lax.all_to_all(reduced, "rows", split_axis=0, concat_axis=0, tiled=True)
    source_ids = lax.dynamic_slice_in_dim(
        pair_list[:, row_index, :], grp_index * share_size, share_size, 1
    )
    local_ids = source_ids.reshape(-1) - row_index * region_size
    select_matrix = (lax.iota(jnp.int32, region_size)[:, None] == local_ids[None, :]).astype(
        jnp.float32
    )
    flat_received = received.reshape(local_ids.shape[0], width * width)
    owner_tiles = jnp.dot(
        select_matrix,
        flat_received,
        precision=lax.Precision.HIGHEST,
        preferred_element_type=jnp.float32,
    )
    owned_tiles = lax.psum_scatter(
        owner_tiles.reshape(region_size, width, width), "grp", scatter_dimension=0, tiled=True
    )
    tile_dev = owned_tiles.shape[0]
    owned_pairs = (row_index * grp_axis_size + grp_index) * tile_dev + lax.iota(jnp.int32, tile_dev)
    owned_blocks = jnp.take(pair_blocks, owned_pairs, axis=0)
    scale_blocks = root_mean.reshape(block_count, width)
    left_scale = jnp.take(scale_blocks, owned_blocks[:, 0], axis=0)
    right_scale = jnp.take(scale_blocks, owned_blocks[:, 1], axis=0)
    return owned_tiles / (sample_count * left_scale[:, :, None] * right_scale[:, None, :])


def solution(mesh):
    in_specs = (P(("rows", "grp"), None), P(("rows", "grp"), None, None), P(), P(), P())
    out_specs = P(("rows", "grp"), None, None)
    return jax.shard_map(shards, mesh=mesh, in_specs=in_specs, out_specs=out_specs, check_vma=False)
```

profile of v0, /device:TPU:1, one launch (start us, length us, event | category | flops | bytes accessed | tf_op | source)
XLA Modules:
  0.0 562.8 jit_solution(3202321126281547467)
XLA Ops:
  7.4 6.8 %multiply_reduce_fusion = f32[16384]{0:T(1024)} fusion(bf16[320,16384]{1,0:T(8,128)(2,1)} %param.13), kind=kLoop, calls=%fused_computation.29 | loop fusion | flops 15712256 | bytes 10551296 | tf_op jit(solution)/shard_map/reduce_sum | solution.py:39
  14.2 0.7 constant_dynamic-slice_fusion.3
  15.1 1.7 gather_fusion.4
  16.9 1.7 gather_fusion.3
  18.8 11.2 %copy.49 = bf16[40,8,128,128]{3,2,1,0:T(8,128)(2,1)} copy(bf16[40,8,128,128]{3,1,2,0:T(8,128)(2,1)} %bitcast.69) | data formatting | bytes 20971520
  30.0 8.4 %convert_reduce_fusion = f32[128,320]{1,0:T(8,128)S(1)} fusion(s32[128,256]{1,0:T(8,128)S(1)} %bitcast.73), kind=kLoop, calls=%fused_computation.27 | loop fusion | flops 31416320 | bytes 294912 | tf_op jit(solution)/shard_map/reduce_sum | solution.py:44
  38.5 10.0 %multiply_convert_fusion = bf16[320,128,128]{2,1,0:T(8,128)(2,1)} fusion(bf16[40,8,128,128]{3,2,1,0:T(8,128)(2,1)} %copy.49, f32[320,128]{1,0:T(8,128)S(1)} %copy.39), kind=kLoop, calls=%fused_computation.30 | loop fusion | flops 15728640 | bytes 21135360 | tf_op jit(solution)/shard_map/convert_element_type | solution.py:48
  48.5 14.7 %copy.40 = bf16[320,128,128]{2,0,1:T(8,128)(2,1)} copy(bf16[320,128,128]{2,1,0:T(8,128)(2,1)} %multiply_convert_fusion) | data formatting | bytes 20971520 | tf_op jit(solution)/shard_map/while | solution.py:67
  63.3 10.9 %copy_bitcast_fusion = bf16[320,128,128]{2,0,1:T(8,128)(2,1)} fusion(bf16[320,16384]{1,0:T(8,128)(2,1)} %param.13), kind=kLoop, calls=%fused_computation.32 | loop fusion | bytes 20971520 | tf_op jit(solution)/shard_map/while | solution.py:67
  74.2 127.8 %while.10 = (s32[]{:T(128)}, f32[8,32,128,128]{3,2,1,0:T(8,128)}, s32[8,32]{1,0:T(8,128)S(1)}, bf16[320,128,128]{2,0,1:T(8,128)(2,1)}, s32[8,32]{1,0:T(8,128)S(1)}, /*index=5*/bf16[320,128,128]{2,0,1:T(8,128)(2,1)}, s32[]{:T(128)}) while((s32[]{:T(128)}, f32[8,32,128,128]{3,2,1,0:T(8,128)}, s32[8,32]{1,0:T(8,128)S(1)}, ...), condition=%wide.region_2.5_spmd, body=%wide.region_1.4_spmd.sunk | while | flops 338168192 | bytes 17835728 | solution.py:67
  74.2 5.1 gather_fusion
  79.3 6.4 %gather_fusion.1 = bf16[32,320,128]{2,1,0:T(8,128)(2,1)} fusion(bf16[320,128,128]{2,0,1:T(8,128)(2,1)} %get-tuple-element.153, s32[1024]{0:T(1024)S(1)} %pad_clamp_fusion.9), kind=kCustom, calls=%fused_computation.1.clone.clone.1 | custom fusion | bytes 5243008 | tf_op jit(solution)/shard_map/while/body/eval_jaxpr/jit(_take)/gather | solution.py:61
  85.7 4.3 bitcast_dynamic-update-slice_fusion.2
  90.0 5.0 gather_fusion
  95.1 6.3 %gather_fusion.1 = bf16[32,320,128]{2,1,0:T(8,128)(2,1)} fusion(bf16[320,128,128]{2,0,1:T(8,128)(2,1)} %get-tuple-element.153, s32[1024]{0:T(1024)S(1)} %pad_clamp_fusion.9), kind=kCustom, calls=%fused_computation.1.clone.clone.1 | custom fusion | bytes 5243008 | tf_op jit(solution)/shard_map/while/body/eval_jaxpr/jit(_take)/gather | solution.py:61
  101.4 4.3 bitcast_dynamic-update-slice_fusion.2
  105.7 5.6 gather_fusion
  111.3 7.0 %gather_fusion.1 = bf16[32,320,128]{2,1,0:T(8,128)(2,1)} fusion(bf16[320,128,128]{2,0,1:T(8,128)(2,1)} %get-tuple-element.153, s32[1024]{0:T(1024)S(1)} %pad_clamp_fusion.9), kind=kCustom, calls=%fused_computation.1.clone.clone.1 | custom fusion | bytes 5243008 | tf_op jit(solution)/shard_map/while/body/eval_jaxpr/jit(_take)/gather | solution.py:61
  118.2 4.3 bitcast_dynamic-update-slice_fusion.2
  122.6 5.7 %gather_fusion = bf16[32,320,128]{2,1,0:T(8,128)(2,1)S(1)} fusion(bf16[320,128,128]{2,0,1:T(8,128)(2,1)} %get-tuple-element.155, s32[1024]{0:T(1024)S(1)} %pad_clamp_fusion.8), kind=kCustom, calls=%fused_computation.4.clone.clone.1 | custom fusion | bytes 5243008 | tf_op jit(solution)/shard_map/while/body/eval_jaxpr/jit(_take)/gather | solution.py:62
  128.3 6.6 %gather_fusion.1 = bf16[32,320,128]{2,1,0:T(8,128)(2,1)} fusion(bf16[320,128,128]{2,0,1:T(8,128)(2,1)} %get-tuple-element.153, s32[1024]{0:T(1024)S(1)} %pad_clamp_fusion.9), kind=kCustom, calls=%fused_computation.1.clone.clone.1 | custom fusion | bytes 5243008 | tf_op jit(solution)/shard_map/while/body/eval_jaxpr/jit(_take)/gather | solution.py:61
  134.9 4.3 bitcast_dynamic-update-slice_fusion.2
  139.2 5.0 gather_fusion
  144.2 6.3 %gather_fusion.1 = bf16[32,320,128]{2,1,0:T(8,128)(2,1)} fusion(bf16[320,128,128]{2,0,1:T(8,128)(2,1)} %get-tuple-element.153, s32[1024]{0:T(1024)S(1)} %pad_clamp_fusion.9), kind=kCustom, calls=%fused_computation.1.clone.clone.1 | custom fusion | bytes 5243008 | tf_op jit(solution)/shard_map/while/body/eval_jaxpr/jit(_take)/gather | solution.py:61
  150.6 4.3 bitcast_dynamic-update-slice_fusion.2
  154.9 5.0 gather_fusion
  160.0 6.3 %gather_fusion.1 = bf16[32,320,128]{2,1,0:T(8,128)(2,1)} fusion(bf16[320,128,128]{2,0,1:T(8,128)(2,1)} %get-tuple-element.153, s32[1024]{0:T(1024)S(1)} %pad_clamp_fusion.9), kind=kCustom, calls=%fused_computation.1.clone.clone.1 | custom fusion | bytes 5243008 | tf_op jit(solution)/shard_map/while/body/eval_jaxpr/jit(_take)/gather | solution.py:61
  166.3 4.3 bitcast_dynamic-update-slice_fusion.2
  170.6 5.0 gather_fusion
  175.6 6.3 %gather_fusion.1 = bf16[32,320,128]{2,1,0:T(8,128)(2,1)} fusion(bf16[320,128,128]{2,0,1:T(8,128)(2,1)} %get-tuple-element.153, s32[1024]{0:T(1024)S(1)} %pad_clamp_fusion.9), kind=kCustom, calls=%fused_computation.1.clone.clone.1 | custom fusion | bytes 5243008 | tf_op jit(solution)/shard_map/while/body/eval_jaxpr/jit(_take)/gather | solution.py:61
  182.0 4.3 bitcast_dynamic-update-slice_fusion.2
  186.3 5.0 gather_fusion
  191.4 6.3 %gather_fusion.1 = bf16[32,320,128]{2,1,0:T(8,128)(2,1)} fusion(bf16[320,128,128]{2,0,1:T(8,128)(2,1)} %get-tuple-element.153, s32[1024]{0:T(1024)S(1)} %pad_clamp_fusion.9), kind=kCustom, calls=%fused_computation.1.clone.clone.1 | custom fusion | bytes 5243008 | tf_op jit(solution)/shard_map/while/body/eval_jaxpr/jit(_take)/gather | solution.py:61
  197.7 4.3 bitcast_dynamic-update-slice_fusion.2
  202.0 6.6 %multiply_bitcast_fusion = f32[4,64,1,128,128]{4,3,0,1,2:T(8,128)S(1)} fusion(f32[64,4,1,128,128]{4,3,1,0,2:T(8,128)} %bitcast.70, f32[64,4]{1,0:T(8,128)S(1)} %fusion.18), kind=kLoop, calls=%fused_computation.31 | loop fusion | flops 4194304 | bytes 33555456 | tf_op jit(solution)/shard_map/transpose | solution.py:19
  208.6 1.8 copy.42
  210.3 185.9 %all_to_all.10 = f32[4,64,1,128,128]{4,3,1,2,0:T(8,128)} all-to-all(f32[4,64,1,128,128]{4,3,1,2,0:T(8,128)S(1)} %copy.42), channel_id=1, replica_groups=mesh['rows'=64,'grp'=4] {'grp'}, dimensions={0} | all-to-all | bytes 33554432 | tf_op jit(solution)/shard_map/all_to_all | solution.py:24
  396.2 10.2 %reduce_sum.39 = f32[64,128,128]{2,1,0:T(8,128)} reduce(f32[4,64,1,128,128]{4,3,1,2,0:T(8,128)} %all_to_all.10, f32[]{:T(128)} %constant.94.clone.1), dimensions={0,2}, to_apply=%region_3.6 | reduce | flops 3145728 | bytes 20971524 | tf_op jit(solution)/shard_map/reduce_sum | solution.py:25
  406.4 15.8 %all-to-all-start.1 = ((f32[64,1,128,128]{3,2,1,0:T(8,128)}), f32[64,1,128,128]{3,2,1,0:T(8,128)}, u32[]{:S(2)}, u32[]{:S(2)}) async-start(f32[64,1,128,128]{3,2,1,0:T(8,128)} %bitcast.71), calls=%async_computation.1 | async-start | bytes 8388608 | tf_op jit(solution)/shard_map/all_to_all | solution.py:73
  422.2 2.2 subtract_reduce_fusion
  424.5 93.6 %all-to-all-done.1 = f32[64,1,128,128]{3,2,1,0:T(8,128)} async-done(((f32[64,1,128,128]{3,2,1,0:T(8,128)}), f32[64,1,128,128]{3,2,1,0:T(8,128)}, u32[]{:S(2)}, u32[]{:S(2)}) %all-to-all-start.1) | async-done | bytes 4194336 | tf_op jit(solution)/shard_map/all_to_all | solution.py:73
  518.0 7.3 %fusion.15 = f32[32,128,128]{2,0,1:T(8,128)} fusion(s32[64]{0:T(128)S(1)} %subtract_reduce_fusion, f32[8,8,128,128]{3,2,1,0:T(8,128)} %bitcast.24), kind=kOutput, calls=%fused_computation.34 | convolution fusion | flops 402655232 | bytes 6291712 | tf_op jit(solution)/shard_map/dot_general | solution.py:82
  525.8 0.6 gather_fusion.2
  526.7 18.3 %reshape.173 = f32[256,16384]{1,0:T(8,128)} reshape(f32[4194304]{0:T(1024)} %all-gather.3.cloned.1.call-done) | data formatting | bytes 33554432 | tf_op jit(solution)/shard_map/all_gather | solution.py:12
  545.0 6.7 %reduce_sum.42 = f32[16384]{0:T(1024)S(1)} reduce(f32[256,16384]{1,0:T(8,128)} %reshape.173, f32[]{:T(128)} %constant.94.clone.1), dimensions={0}, to_apply=%region_6.9 | reduce | flops 4177920 | bytes 16842756 | tf_op jit(solution)/shard_map/reduce_sum | solution.py:13
  551.8 0.6 gather_fusion.5
  553.2 1.2 multiply_divide_fusion
  554.4 0.9 copy.46
  (66 shorter events, 2.4 us)
Async XLA Ops:
  7.4 55.9 %copy-start = (s32[64,64]{1,0:T(8,128)S(1)}, s32[64,64]{1,0:T(8,128)}, u32[]{:S(2)}) copy-start(s32[64,64]{1,0:T(8,128)} %param.16) | copy-start | bytes 49156
  7.4 7.7 %copy-start.3 = (s32[2048,2]{0,1:T(2,128)S(1)}, s32[2048,2]{0,1:T(2,128)}, u32[]{:S(2)}) copy-start(s32[2048,2]{0,1:T(2,128)} %param.17) | copy-start | bytes 49156
  7.4 519.3 %all-gather.3.cloned.1.call-start = ((), (), s32[]{:S(2)}) async-start(), calls=%async_computation.4 | async-start | bytes 16842752 | tf_op jit(solution)/shard_map/all_gather | solution.py:12
  18.8 11.2 %copy-start.2 = (s32[1,128,256]{2,1,0:T(8,128)S(1)}, s32[1,128,256]{2,1,0:T(8,128)}, u32[]{:S(2)}) copy-start(s32[1,128,256]{2,1,0:T(8,128)} %param.14) | copy-start | bytes 393220
  406.4 111.6 %all-to-all-start.1 = ((f32[64,1,128,128]{3,2,1,0:T(8,128)}), f32[64,1,128,128]{3,2,1,0:T(8,128)}, u32[]{:S(2)}, u32[]{:S(2)}) async-start(f32[64,1,128,128]{3,2,1,0:T(8,128)} %bitcast.71), calls=%async_computation.1 | async-start | bytes 8388608 | tf_op jit(solution)/shard_map/all_to_all | solution.py:73
  422.2 131.0 %reduce-scatter.2.cloned.1.call-start = ((), (), s32[]{:S(2)}) async-start(), calls=%async_computation.3 | async-start | bytes 2621440 | tf_op jit(solution)/shard_map/reduce_scatter | solution.py:88
  526.7 28.6 %copy-start.1 = (s32[64,64]{1,0:T(8,128)S(1)}, s32[64,64]{1,0:T(8,128)}, u32[]{:S(2)}) copy-start(s32[64,64]{1,0:T(8,128)} %param.16) | copy-start | bytes 49156
Sparse Core Ops, SparseCore 0:
  14.3 129.3 all-gather.2
Sparse Core Ops, SparseCore 1:
  525.5 26.5 reduce-scatter.1
where the time goes:
time: 565 us; the launch traced here: 563 us
  blocking collectives  186 us (33%)
  local copies, waits for them, and re-layouts  158 us (28%)
  waiting for transfers between devices  93.6 us (17%)
  other arithmetic  52.7 us (9%)
  matrix products  41.7 us (7%)
  starting transfers between devices  15.8 us (3%)
  between operations  15.1 us (3%)
    all_to_all x1, blocking collectives, summed_on_arrival(): lax.all_to_all(pieces, axis, split_axis=0, concat_axis=0, tiled=True)  186 us
    all_to_all x1, waiting for transfers between devices, shards(): lax.all_to_all(reduced, 'rows', split_axis=0, concat_axis=0, tiled=True)  93.6 us
    gather x8, local copies, waits for them, and re-layouts, tile_group(): weighted_cols = jnp.take(weighted, block_pair[0], axis=1)  51.5 us
    gather x8, local copies, waits for them, and re-layouts, tile_group(): plain_cols = jnp.take(blocks, block_pair[1], axis=1)  41.5 us
    dot_general x8, matrix products, tile_group(): jnp.einsum('rgi,rgj->gij', weighted_cols, plain_cols, preferred_element_t...  34.4 us
    while x2, local copies, waits for them, and re-layouts, shards(): partial_tiles = lax.map(tile_group, (first_block, second_block))  25.6 us
    all_gather x1, local copies, waits for them, and re-layouts, total_of_pieces(): pieces = lax.all_gather(x, axis)  18.3 us
    all_to_all x1, starting transfers between devices, shards(): lax.all_to_all(reduced, 'rows', split_axis=0, concat_axis=0, tiled=True)  15.8 us
  transfers between devices with their start and end apart: 3, of which 1 were waited for; matrix products, arithmetic and copies ran while one was open for 43% of the time, Pallas kernels for 0%

commit v1 on v0

v1 whole, which is shorter than its diff:
```python
import functools

import jax
import jax.numpy as jnp
from jax import lax
from jax.experimental import pallas as pl
from jax.experimental.pallas import tpu as pltpu
from jax.sharding import PartitionSpec as P

MESH = pl.DeviceIdType.MESH
epsilon = 1e-06
ROWS = 320
PADDED = 384
COLS = 16384
BLOCKS = 128
SAMPLES = 256
SLOTS = 256
CHUNKS = 4
Y_LANES = 37
UNROLL = 8
GROUPS = 8
FIRST, SECOND, PLACE, DENSE, OWNED, SPARE = 0, 256, 512, 768, 2816, 2832
TABLE = 2840
SMALL_CAP = 192


def prep_kernel(
    all_lists_ref, all_counts_ref, counts_vmem_ref, blocks_ref, picked_ref,
    table_ref, mult_ref, fits_ref, turned_ref, lists_ref, counts_ref, sem,
):
    s = lax.axis_index("rows")
    g = lax.axis_index("grp")
    me = lax.rem(s, 16)
    near = pl.ds((s // 16) * 16, 16)
    copies = (
        pltpu.make_async_copy(all_lists_ref.at[near], lists_ref, sem.at[0]),
        pltpu.make_async_copy(all_counts_ref.at[near], counts_ref, sem.at[1]),
    )
    for copy in copies:
        copy.start()
    turned_ref[...] = picked_ref[0].T
    most = jnp.max(jnp.sum(counts_vmem_ref[...], axis=1, keepdims=True))
    fits_ref[0] = (most <= SMALL_CAP).astype(jnp.int32)
    rows = lax.broadcasted_iota(jnp.int32, (128, 128), 0)
    zero = jnp.zeros((128, 128), jnp.int32)

    def clear(j, total):
        table_ref[FIRST + j] = 0
        table_ref[SECOND + j] = 0
        for i in range(8):
            table_ref[DENSE + j * 8 + i] = 64
        row = turned_ref[pl.ds(j, 1), :]
        return total + jnp.where(row == rows, 1, 0)

    total = lax.fori_loop(0, SAMPLES, clear, zero, unroll=4)
    mult_ref[:, 0, 0:128] = total.astype(jnp.float32).T

    for copy in copies:
        copy.wait()

    def compact(t, carry):
        pos, second, third = carry
        for x in range(4):
            r = x * 16 + t
            count = counts_ref[me, r]
            count_in = counts_ref[t, x * 16 + me]
            for k in range(4):
                j = t * 16 + x * 4 + k
                pair = lists_ref[me, k, r]
                live = k < count
                table_ref[FIRST + pos] = blocks_ref[0, pair]
                table_ref[SECOND + pos] = blocks_ref[1, pair]
                table_ref[PLACE + x * 64 + t * 4 + k] = jnp.where(live, pos, 0)
                pos = jnp.where(live, jnp.minimum(pos + 1, SLOTS - 1), pos)
                local = lists_ref[t, k, x * 16 + me] - (x * 16 + me) * 32
                place = DENSE + (x * 32 + local) * 16 + t
                table_ref[jnp.where(k < count_in, place, SPARE)] = t * 4 + k
                row = turned_ref[pl.ds(j, 1), :]
                second = second + jnp.where(row == rows + 128, 1, 0)
                third = third + jnp.where(row == rows + 256, 1, 0)
        return pos, second, third

    _, second, third = lax.fori_loop(0, 16, compact, (jnp.int32(0), zero, zero))
    mult_ref[:, 0, 128:256] = second.astype(jnp.float32).T
    mult_ref[:, 0, 256:384] = third.astype(jnp.float32).T

    def owned(i, carry):
        pair = (s * 4 + g) * 8 + i
        table_ref[OWNED + 2 * i] = blocks_ref[0, pair]
        table_ref[OWNED + 2 * i + 1] = blocks_ref[1, pair]
        return carry

    lax.fori_loop(0, 8, owned, 0)


def main_kernel(n, table_ref, mult_ref, matrix_ref, raw_ref, square_ref, *scratch):
    half = n // 2
    names = iter(scratch)
    mat = next(names)
    tiles = next(names)
    r1p = [next(names) for _ in range(CHUNKS)]
    r1m = [next(names) for _ in range(CHUNKS)]
    r2p = [next(names) for _ in range(CHUNKS)]
    r2m = [next(names) for _ in range(CHUNKS)]
    zs = [next(names) for _ in range(CHUNKS)]
    zr = [[next(names) for _ in range(4)] for _ in range(CHUNKS)]
    dn = [next(names) for _ in range(CHUNKS)]
    x1p = [next(names) for _ in range(CHUNKS)]
    x1m = [next(names) for _ in range(CHUNKS)]
    x2p = [next(names) for _ in range(CHUNKS)]
    x2m = [next(names) for _ in range(CHUNKS)]
    fin = [next(names) for _ in range(CHUNKS)]
    gathered = next(names)
    sq, qy, q1, qx, q2, qz, g1, g2 = [next(names) for _ in range(8)]
    load_sem = next(names)
    ysend, yrecv = next(names), next(names)
    zsend, zrecv = next(names), next(names)
    xsend, xrecv = next(names), next(names)
    fsend, frecv = next(names), next(names)
    qsend, qrecv = next(names), next(names)

    s = lax.axis_index("rows")
    y = lax.axis_index("grp")
    x = s // 16
    me = lax.rem(s, 16)
    yp, ym, yo = lax.rem(y + 1, 4), lax.rem(y + 3, 4), lax.rem(y + 2, 4)
    xp, xm, xo = lax.rem(x + 1, 4), lax.rem(x + 3, 4), lax.rem(x + 2, 4)

    def at_y(o):
        return (s, lax.rem(y + o, 4))

    def at_x(o):
        return (lax.rem(x + o, 4) * 16 + me, y)

    def at_z(o):
        return (x * 16 + lax.rem(me + o, 16), y)

    def load(b, carry):
        cols = pl.ds(pl.multiple_of(b * 128, 128), 128)
        pltpu.make_async_copy(matrix_ref.at[:, cols], mat.at[b, pl.ds(0, ROWS)], load_sem).start()
        return carry

    lax.fori_loop(0, BLOCKS, load, 0)

    barrier = pltpu.get_barrier_semaphore()
    for o in range(1, 4):
        pl.semaphore_signal(barrier, inc=1, device_id=at_y(o), device_id_type=MESH)
        pl.semaphore_signal(barrier, inc=1, device_id=at_x(o), device_id_type=MESH)
    for o in range(1, 16):
        pl.semaphore_signal(barrier, inc=1, device_id=at_z(o), device_id_type=MESH)

    def clear(b, carry):
        mat[b, pl.ds(ROWS, PADDED - ROWS)] = jnp.zeros((PADDED - ROWS, 128), jnp.bfloat16)
        return carry

    lax.fori_loop(0, BLOCKS, clear, 0, unroll=4)
    for u in range(CHUNKS):
        for step in range(4):
            zr[u][step][64] = jnp.zeros((8, 128), jnp.float32)
    whole = mat.at[:, pl.ds(0, ROWS)]
    pltpu.make_async_copy(whole, whole, load_sem).wait()

    def tile(j, carry):
        b = table_ref[FIRST + j]
        c = table_ref[SECOND + j]
        left = mat[b].T
        right = mat[c]
        weight = mult_ref[b]
        weighted = left * weight.astype(jnp.bfloat16)
        out = jnp.dot(weighted, right, preferred_element_type=jnp.float32)
        tiles[:, j] = out.reshape(16, 8, 128)
        return carry

    lanes = iter(range(Y_LANES))

    def y_copies(u, quarter, sources, target, o):
        copies = []
        for start, size, shift in sources:
            lane = next(lanes)
            copies.append(
                pltpu.make_async_remote_copy(
                    src_ref=tiles.at[quarter * CHUNKS + u, pl.ds(start, size)],
                    dst_ref=target.at[pl.ds(start - shift, size)],
                    send_sem=ysend.at[lane],
                    recv_sem=yrecv.at[lane],
                    device_id=at_y(o),
                    device_id_type=MESH,
                )
            )
        return copies

    group_size = n // GROUPS
    split = GROUPS // 2
    first_up, first_down, plain_up, plain_down, summed_up, summed_down = [], [], [], [], [], []
    for u in range(CHUNKS):
        count = split if u == 0 else 1
        size = half // count
        low = [(i * size, size, 0) for i in range(count)]
        high = [(half + i * size, size, 0) for i in range(count)]
        high_moved = [(start, size, half) for start, size, _ in high]
        if u == 1:
            high_moved = [(half, half // 2, half), (half + half // 2, half // 2, half)]
        first_up.append(y_copies(u, yo, low, r1p[u], 1))
        first_down.append(y_copies(u, yo, high_moved, r1m[u], 3))
        plain_up.append(y_copies(u, yp, high, r2p[u], 1))
        plain_down.append(y_copies(u, ym, low, r2m[u], 3))
        summed_up.append(y_copies(u, yp, [(0, half, 0)], r2p[u], 1))
        summed_down.append(y_copies(u, ym, [(half, half, 0)], r2m[u], 3))
    every_y = [c for kind in (first_up, first_down, plain_up, plain_down, summed_up, summed_down) for part in kind for c in part]

    def begin(*copies):
        for copy in copies:
            copy.start()

    def tiles_of(group):
        lax.fori_loop(group * group_size, (group + 1) * group_size, tile, 0, unroll=UNROLL)

    def add_up(u):
        for copy in first_up[u]:
            copy.wait_recv()

        def body(i, carry):
            tiles[yp * CHUNKS + u, i] = tiles[yp * CHUNKS + u, i] + r1p[u][i]
            return carry

        lax.fori_loop(0, half, body, 0, unroll=8)
        begin(*summed_up[u])

    def add_down(u):
        for copy in first_down[u]:
            copy.wait_recv()

        def body(i, carry):
            tiles[ym * CHUNKS + u, half + i] = tiles[ym * CHUNKS + u, half + i] + r1m[u][i]
            return carry

        lax.fori_loop(0, half, body, 0, unroll=8)
        begin(*summed_down[u])

    tiles_of(0)
    pl.semaphore_wait(barrier, 21)
    begin(first_up[0][0], plain_down[0][0])
    for i in range(1, split):
        tiles_of(i)
        begin(first_up[0][i], plain_down[0][i])
    for i in range(split):
        tiles_of(split + i)
        begin(first_down[0][i], plain_up[0][i])
        if i == split - 2:
            add_up(0)
    begin(first_down[1][0], *first_up[1])

    def squares(i, carry):
        for part in range(8):
            b = i * 8 + part

            def step(r, total):
                v = mat[b, pl.ds(pl.multiple_of(r * 32, 32), 32)].astype(jnp.float32)
                return total + v * v

            total = lax.fori_loop(0, ROWS // 32, step, jnp.zeros((32, 128), jnp.float32), unroll=True)
            sq[i, pl.ds(part, 1), :] = jnp.sum(total, axis=0, keepdims=True)
        return carry

    lax.fori_loop(0, 16, squares, 0)

    def q_copy(step, src, dst, device):
        return pltpu.make_async_remote_copy(
            src_ref=src,
            dst_ref=dst,
            send_sem=qsend.at[step],
            recv_sem=qrecv.at[step],
            device_id=device,
            device_id_type=MESH,
        )

    def q_wait(step, ref):
        pltpu.make_async_copy(ref, ref, qrecv.at[step]).wait()

    for o in range(1, 4):
        q_copy(0, sq.at[pl.ds(lax.rem(y + o, 4) * 4, 4)], qy.at[o - 1], at_y(o)).start()

    def z_send(u):
        for kind in (plain_up, plain_down, summed_up, summed_down):
            for copy in kind[u]:
                copy.wait_recv()

        for step, block in enumerate((xo, xp, xm, x)):

            def gather(i, carry, step=step, block=block):
                place = table_ref[PLACE + block * 64 + i]
                zs[u][step * 64 + i] = tiles[y * CHUNKS + u, place] + r2p[u][place] + r2m[u][place]
                return carry

            lax.fori_loop(0, 64, gather, 0, unroll=8)

            def send(o, carry, step=step):
                there = lax.rem(me + o, 16)
                pltpu.make_async_remote_copy(
                    src_ref=zs[u].at[pl.ds(step * 64 + there * 4, 4)],
                    dst_ref=zr[u][step].at[pl.ds(me * 4, 4)],
                    send_sem=zsend.at[u, step],
                    recv_sem=zrecv.at[u, step],
                    device_id=at_z(o),
                    device_id_type=MESH,
                ).start()
                return carry

            lax.fori_loop(1, 16, send, 0)
            zr[u][step][pl.ds(me * 4, 4)] = zs[u][pl.ds(step * 64 + me * 4, 4)]

    def x_copy(u, lane, src, dst, o):
        return pltpu.make_async_remote_copy(
            src_ref=src,
            dst_ref=dst,
            send_sem=xsend.at[u, lane],
            recv_sem=xrecv.at[u, lane],
            device_id=at_x(o),
            device_id_type=MESH,
        )

    x_copies = []
    for u in range(CHUNKS):
        x_copies.append(
            (
                x_copy(u, 0, dn[u].at[pl.ds(xo * 32, 16)], x1p[u], 1),
                x_copy(u, 1, dn[u].at[pl.ds(xo * 32 + 16, 16)], x1m[u], 3),
                x_copy(u, 2, dn[u].at[pl.ds(xp * 32, 32)], x2p[u], 1),
                x_copy(u, 3, dn[u].at[pl.ds(xm * 32, 32)], x2m[u], 3),
            )
        )

    blocks = (xo, xp, xm, x)

    def dense(u, step):
        landed = zs[u].at[pl.ds(0, 60)]
        pltpu.make_async_copy(landed, landed, zrecv.at[u, step]).wait()
        block = blocks[step]

        def body(i, carry):
            p = block * 32 + i
            parts = [zr[u][step][table_ref[DENSE + p * 16 + src]] for src in range(16)]
            while len(parts) > 1:
                parts = [a + b for a, b in zip(parts[::2], parts[1::2])]
            dn[u][p] = parts[0]
            return carry

        lax.fori_loop(0, 32, body, 0, unroll=2)

    def z_finish(u):
        dense(u, 0)
        begin(x_copies[u][0], x_copies[u][1])
        for step in (1, 2, 3):
            dense(u, step)

    def x_second(u):
        x_copies[u][0].wait_recv()
        x_copies[u][1].wait_recv()
        up, down = pl.ds(xp * 32, 16), pl.ds(xm * 32 + 16, 16)
        dn[u][up] = dn[u][up] + x1p[u][...]
        dn[u][down] = dn[u][down] + x1m[u][...]
        x_copies[u][2].start()
        x_copies[u][3].start()

    def x_finish(u):
        x_copies[u][2].wait_recv()
        x_copies[u][3].wait_recv()
        fin[u][...] = dn[u][pl.ds(x * 32, 32)] + x2p[u][...] + x2m[u][...]
        for o in range(1, 4):
            pltpu.make_async_remote_copy(
                src_ref=fin[u].at[pl.ds(lax.rem(y + o, 4) * 8, 8)],
                dst_ref=gathered.at[y * CHUNKS + u],
                send_sem=fsend.at[u],
                recv_sem=frecv.at[u],
                device_id=at_y(o),
                device_id_type=MESH,
            ).start()
        gathered[y * CHUNKS + u] = fin[u][pl.ds(y * 8, 8)]

    add_down(0)
    begin(first_down[1][1], *plain_up[1], *plain_down[1])
    z_send(0)
    q_wait(0, qy)
    q1[...] = sq[pl.ds(y * 4, 4)] + qy[0] + qy[1] + qy[2]
    for o in range(1, 4):
        q_copy(1, q1.at[lax.rem(x + o, 4)], qx.at[o - 1], at_x(o)).start()
    add_up(1)
    add_down(1)
    begin(*first_up[2], *first_down[2], *plain_up[2], *plain_down[2])
    q_wait(1, qx)
    q2[...] = q1[x] + qx[0] + qx[1] + qx[2]
    for o in range(1, 16):
        q_copy(2, q2, qz.at[o - 1], at_z(o)).start()
    z_send(1)
    z_finish(0)
    add_up(2)
    add_down(2)
    begin(*first_up[3], *first_down[3], *plain_up[3], *plain_down[3])
    q_wait(2, qz)
    total = q2[...]
    for o in range(15):
        total = total + qz[o]
    g1[x] = total
    for o in range(1, 4):
        q_copy(3, g1.at[x], g1.at[x], at_x(o)).start()
    z_send(2)
    z_finish(1)
    add_up(3)
    add_down(3)
    x_second(0)
    pltpu.make_async_copy(g1.at[pl.ds(0, 3)], g1.at[pl.ds(0, 3)], qrecv.at[3]).wait()
    for o in range(1, 4):
        q_copy(4, g1, g2.at[pl.ds(y * 4, 4)], at_y(o)).start()
    g2[pl.ds(y * 4, 4)] = g1[...]
    z_send(3)
    x_finish(0)
    z_finish(2)
    x_second(1)
    x_finish(1)
    x_second(2)
    x_finish(2)
    dense(3, 0)
    begin(x_copies[3][0], x_copies[3][1])
    dense(3, 1)
    dense(3, 2)
    x_second(3)
    dense(3, 3)
    x_finish(3)

    pltpu.make_async_copy(g2.at[pl.ds(0, 12)], g2.at[pl.ds(0, 12)], qrecv.at[4]).wait()
    square_ref[...] = g2[...]
    for u in range(CHUNKS):
        piece = gathered.at[pl.ds(0, 3)]
        pltpu.make_async_copy(piece, piece, frecv.at[u]).wait()
    raw_ref[...] = gathered[...]

    for copy in every_y:
        copy.wait_send()
    for u in range(CHUNKS):
        for step in range(4):
            piece = zs[u].at[pl.ds(0, 60)]
            pltpu.make_async_copy(piece, piece, zsend.at[u, step]).wait()
        for copy in x_copies[u]:
            copy.wait_send()
        piece = fin[u].at[pl.ds(0, 24)]
        pltpu.make_async_copy(piece, piece, fsend.at[u]).wait()
    for step, ref in ((0, qy), (1, qx), (2, qz), (3, g1.at[pl.ds(0, 3)]), (4, g2.at[pl.ds(0, 12)])):
        pltpu.make_async_copy(ref, ref, qsend.at[step]).wait()


def finish_kernel(table_ref, raw_ref, square_ref, out_ref, scale_ref):
    scale_ref[...] = jnp.sqrt(square_ref[...] / (ROWS * 256) + epsilon)
    for p in range(8):
        b = table_ref[OWNED + 2 * p]
        c = table_ref[OWNED + 2 * p + 1]
        left = jnp.broadcast_to(scale_ref[pl.ds(b, 1), :], (128, 128)).T
        right = scale_ref[pl.ds(c, 1), :]
        value = raw_ref[:, p].reshape(128, 128)
        out_ref[p] = value / (SAMPLES * left * right)


def vmem():
    return pl.BlockSpec(memory_space=pltpu.VMEM)


def smem():
    return pl.BlockSpec(memory_space=pltpu.SMEM)


def main_call(n, collective, table, mult, matrix):
    half = n // 2

    def tile_buffer(*lead):
        return pltpu.VMEM((*lead, 8, 128), jnp.float32)

    scratch = [pltpu.VMEM((BLOCKS, PADDED, 128), jnp.bfloat16), tile_buffer(16, n)]
    for shape in ((half,), (half,), (n,), (n,), (SLOTS,)):
        scratch += [tile_buffer(*shape) for _ in range(CHUNKS)]
    scratch += [tile_buffer(65) for _ in range(CHUNKS * 4)]
    for shape in ((128,), (16,), (16,), (32,), (32,), (32,)):
        scratch += [tile_buffer(*shape) for _ in range(CHUNKS)]
    scratch += [tile_buffer(16, 8)]
    scratch += [tile_buffer(16), tile_buffer(3, 4), tile_buffer(4), tile_buffer(3)]
    scratch += [tile_buffer(), tile_buffer(15), tile_buffer(4), tile_buffer(16)]
    dma = pltpu.SemaphoreType.DMA
    scratch += [dma]
    for shape in ((Y_LANES,), (CHUNKS, 4), (CHUNKS, 4), (CHUNKS,), (5,)):
        scratch += [dma(shape), dma(shape)]
    return pl.pallas_call(
        functools.partial(main_kernel, n),
        out_shape=(
            jax.ShapeDtypeStruct((16, 8, 8, 128), jnp.float32),
            jax.ShapeDtypeStruct((16, 8, 128), jnp.float32),
        ),
        in_specs=[smem(), vmem(), pl.BlockSpec(memory_space=pl.ANY)],
        out_specs=(vmem(), vmem()),
        scratch_shapes=scratch,
        compiler_params=pltpu.CompilerParams(
            collective_id=collective, has_side_effects=True, vmem_limit_bytes=67043328
        ),
        name=f"tiles_{n}",
    )(table, mult, matrix)


def shards(matrix, sample_rows, pair_list, pair_count, pair_blocks):
    table, mult, fits = pl.pallas_call(
        prep_kernel,
        out_shape=(
            jax.ShapeDtypeStruct((TABLE,), jnp.int32),
            jax.ShapeDtypeStruct((BLOCKS, 1, PADDED), jnp.float32),
            jax.ShapeDtypeStruct((1,), jnp.int32),
        ),
        in_specs=[pl.BlockSpec(memory_space=pl.ANY)] * 2 + [vmem(), smem(), vmem()],
        out_specs=(smem(), vmem(), smem()),
        scratch_shapes=[
            pltpu.VMEM((SAMPLES, BLOCKS), jnp.int32),
            pltpu.SMEM((16, 4, 64), jnp.int32),
            pltpu.SMEM((16, 64), jnp.int32),
            pltpu.SemaphoreType.DMA((2,)),
        ],
        name="prep",
    )(jnp.swapaxes(pair_list, 1, 2), pair_count, pair_count, pair_blocks.T, sample_rows)
    raw, square = lax.cond(
        fits[0] > 0,
        functools.partial(main_call, SMALL_CAP, 1),
        functools.partial(main_call, SLOTS, 2),
        table,
        mult,
        matrix,
    )
    return pl.pallas_call(
        finish_kernel,
        out_shape=jax.ShapeDtypeStruct((8, 128, 128), jnp.float32),
        in_specs=[smem(), vmem(), vmem()],
        out_specs=vmem(),
        scratch_shapes=[pltpu.VMEM((BLOCKS, 128), jnp.float32)],
        name="finish",
    )(table, raw, square.reshape(BLOCKS, 128))


def solution(mesh):
    in_specs = (P(("rows", "grp"), None), P(("rows", "grp"), None, None), P(), P(), P())
    out_specs = P(("rows", "grp"), None, None)
    return jax.shard_map(shards, mesh=mesh, in_specs=in_specs, out_specs=out_specs, check_vma=False)
```

time: 565 us -> 162 us (0.29)
  blocking collectives: 186 us -> 0 us
  Pallas kernels: 0 us -> 161 us
  local copies, waits for them, and re-layouts: 158 us -> 0 us
  waiting for transfers between devices: 93.6 us -> 0 us
  other arithmetic: 52.7 us -> 0 us
  matrix products: 41.7 us -> 0 us
  starting transfers between devices: 15.8 us -> 0 us
  between operations: 15.1 us -> 0.64 us
    all_to_all x1 -> x0, blocking collectives: 186 us -> none  [summed_on_arrival(): lax.all_to_all(pieces, axis, split_axis=0, concat_axis=0, tiled=True)]
    pallas_call x0 -> x3, Pallas kernels: none -> 161 us  [the longest x1 151 us: main_call(): pl.pallas_call(functools.partial(main_kernel, n), out_shape=(jax.ShapeDty...]
    gather x21 -> x0, local copies, waits for them, and re-layouts: 98.1 us -> none  [the longest x8 51.5 us: tile_group(): weighted_cols = jnp.take(weighted, block_pair[0], axis=1)]
    all_to_all x1 -> x0, waiting for transfers between devices: 93.6 us -> none  [shards(): lax.all_to_all(reduced, 'rows', split_axis=0, concat_axis=0, tiled=True)]
    dot_general x9 -> x0, matrix products: 41.7 us -> none  [the longest x8 34.4 us: tile_group(): jnp.einsum('rgi,rgj->gij', weighted_cols, plain_cols, preferred_element_t...]
    reduce_sum x4 -> x0, other arithmetic: 32.1 us -> none  [the longest x1 10.2 us: summed_on_arrival(): return arrived.sum(axis=0)]
    while x2 -> x0, local copies, waits for them, and re-layouts: 25.6 us -> none  [shards(): partial_tiles = lax.map(tile_group, (first_block, second_block))]
    all_gather x1 -> x0, local copies, waits for them, and re-layouts: 18.3 us -> none  [total_of_pieces(): pieces = lax.all_gather(x, axis)]
  transfers between devices with their start and end apart: 3 -> 0, of which waited for: 1 -> 0; matrix products, arithmetic and copies ran while one was open for 43% -> 0% of each run, Pallas kernels for 0% -> 0%
where the time goes in v1:
time: 162 us
  Pallas kernels  161 us (99%)
    pallas_call x1, Pallas kernels, main_call(): pl.pallas_call(functools.partial(main_kernel, n), out_shape=(jax.ShapeDty...  151 us
    pallas_call x1, Pallas kernels, shards(): pl.pallas_call(prep_kernel, out_shape=(jax.ShapeDtypeStruct((TABLE,), jnp...  8.1 us

profile of v1, /device:TPU:1, one launch (start us, length us, event | category | flops | bytes accessed | tf_op | source)
XLA Modules:
  0.0 162.0 jit_solution(17542683616549035359)
XLA Ops:
  0.0 8.1 %prep.1 = (s32[2840]{0:T(1024)}, f32[128,1,384]{2,1,0:T(1,128)}, s32[1]{0:T(128)}) custom-call(s32[64,4,64]{2,1,0:T(4,128)} %bitcast.5, s32[64,64]{1,0:T(8,128)} %counts_vmem_ref.1, s32[64,64]{1,0:T(8,128)} %counts_vmem_ref.1, s32[2,2048]{1,0:T(2,128)} %bitcast.8, s32[1,128,256]{2,1,0:T(8,128)} %picked_ref.1), custom_call_target="tpu_custom_call" | custom-call | tf_op jit(solution)/shard_map/prep/pallas_call | solution.py:506
  8.7 151.2 %conditional.1 = (f32[16,8,8,128]{3,2,1,0:T(8,128)}, f32[128,128]{1,0:T(8,128)}) conditional(s32[]{:T(128)} %bitcast.4, (s32[2840]{0:T(1024)}, f32[128,1,384]{2,1,0:T(1,128)}, bf16[320,16384]{1,0:T(8,128)(2,1)}) %tuple.15, (s32[2840]{0:T(1024)}, f32[128,1,384]{2,1,0:T(1,128)}, bf16[320,16384]{1,0:T(8,128)(2,1)}) %tuple.15), branch_computations={%region_0.0_spmd, %region_1.0_spmd} | conditional | bytes 16 | solution.py:523
  8.9 151.0 %tiles_192.1 = (f32[16,8,8,128]{3,2,1,0:T(8,128)}, f32[16,8,128]{2,1,0:T(8,128)}) custom-call(s32[2840]{0:T(1024)} %get-tuple-element.27.table_ref, f32[128,1,384]{2,1,0:T(1,128)} %get-tuple-element.28.mult_ref, bf16[320,16384]{1,0:T(8,128)(2,1)} %get-tuple-element.29.matrix_ref), custom_call_target="tpu_custom_call" | custom-call | tf_op jit(solution)/shard_map/cond/branch_1_fun/tiles_192/pallas_call | solution.py:489
  160.0 2.1 %finish.1 = f32[8,128,128]{2,1,0:T(8,128)} custom-call(s32[2840]{0:T(1024)} %get-tuple-element.37.table_ref, f32[16,8,8,128]{3,2,1,0:T(8,128)} %get-tuple-element.40.raw_ref, f32[128,128]{1,0:T(8,128)} %get-tuple-element.41.square_ref), custom_call_target="tpu_custom_call" | custom-call | tf_op jit(solution)/shard_map/finish/pallas_call | solution.py:531
